TPU v7x, 8 devices: a whole 2x2x1 slice. The times are simulated.
8 devices in a mesh: data: 8 (over z, y, x, core).
Axes of the slice: x: 2, y: 2, z: 1, core: 2. Of those that a mesh axis runs over, the one named last changes fastest.
Arguments:
- w_one: float32 [32, 512, 1024], P(None, 'data')
- w_two: float32 [32, 1024, 512], P(None, 'data')
- mom_one: float32 [32, 512, 1024], P(None, 'data')
- mom_two: float32 [32, 1024, 512], P(None, 'data')
- x_zero: bfloat16 [12288, 512], P('data')
- y_zero: bfloat16 [12288, 512], P('data')
- x_one: bfloat16 [12288, 512], P('data')
- y_one: bfloat16 [12288, 512], P('data')
Outputs:
- output 1: float32 [32, 512, 1024], P(None, 'data')
- output 2: float32 [32, 1024, 512], P(None, 'data')
- output 3: float32 [32, 512, 1024], P(None, 'data')
- output 4: float32 [32, 1024, 512], P(None, 'data')
- output 5: float32 [12288], P('data')
- output 6: float32 [12288, 512], P('data')
All inputs are finite; a program needn't handle non-finite values.
Results may differ from a plain program's by a relative error of at most 0.00859125.
Values are sent between devices in bfloat16 or wider.
A program may use at most 1 GiB of HBM per device.

v0:
```python
import jax
import jax.numpy as jnp
from jax import lax
from jax.sharding import PartitionSpec as P

LEARN_RATE = 0.1
MOMENTUM = 0.9


def run_stack(w_one_b, w_two_b, h_cur):
    saved_vals = []
    for layer_idx in range(w_one_b.shape[0]):
        act_in = h_cur.astype(jnp.bfloat16)
        pre_act = jnp.dot(act_in, w_one_b[layer_idx], preferred_element_type=jnp.float32)
        hidden, gelu_back = jax.vjp(jax.nn.gelu, pre_act)
        hidden = hidden.astype(jnp.bfloat16)
        h_cur = h_cur + jnp.dot(hidden, w_two_b[layer_idx], preferred_element_type=jnp.float32)
        saved_vals.append((act_in, hidden, gelu_back))
    return h_cur, saved_vals


def layer_grads(d_state, w_out, layer_vals):
    act_in, hidden, gelu_back = layer_vals
    d_low = d_state.astype(jnp.bfloat16)
    grad_out = jnp.einsum("tf,td->fd", hidden, d_low, preferred_element_type=jnp.float32).astype(jnp.bfloat16)
    d_hidden = jnp.einsum("td,fd->tf", d_low, w_out, preferred_element_type=jnp.float32)
    d_pre = gelu_back(d_hidden)[0].astype(jnp.bfloat16)
    grad_in = jnp.einsum("td,tf->df", act_in, d_pre, preferred_element_type=jnp.float32).astype(jnp.bfloat16)
    return grad_in, grad_out, d_pre


def solution(mesh):
    n_dev = mesh.shape["data"]
    w_spec = P(None, "data", None)
    row_spec = P("data", None)

    def device_step(w_one, w_two, mom_one, mom_two, x_zero, y_zero, x_one, y_one):
        layers = w_one.shape[0]
        tok_dev, d_model = x_zero.shape
        w_one_b = lax.all_gather(w_one.astype(jnp.bfloat16), "data", axis=1, tiled=True)
        w_two_b = lax.all_gather(w_two.astype(jnp.bfloat16), "data", axis=1, tiled=True)
        h_end, saved_vals = run_stack(w_one_b, w_two_b, x_zero.astype(jnp.float32))
        d_state = (h_end - y_zero.astype(jnp.float32)) / (n_dev * tok_dev * d_model)
        shard_in = [None] * layers
        shard_out = [None] * layers
        for layer_idx in reversed(range(layers)):
            grad_in, grad_out, d_pre = layer_grads(d_state, w_two_b[layer_idx], saved_vals[layer_idx])
            shard_out[layer_idx] = lax.psum_scatter(grad_out, "data", scatter_dimension=0, tiled=True)
            shard_in[layer_idx] = lax.psum_scatter(grad_in, "data", scatter_dimension=0, tiled=True)
            if layer_idx > 0:
                d_state = d_state + jnp.einsum("tf,df->td", d_pre, w_one_b[layer_idx], preferred_element_type=jnp.float32)
        new_mom_one = MOMENTUM * mom_one + jnp.stack(shard_in).astype(jnp.float32)
        new_mom_two = MOMENTUM * mom_two + jnp.stack(shard_out).astype(jnp.float32)
        new_w_one = w_one - LEARN_RATE * new_mom_one
        new_w_two = w_two - LEARN_RATE * new_mom_two
        next_one_b = lax.all_gather(new_w_one.astype(jnp.bfloat16), "data", axis=1, tiled=True)
        next_two_b = lax.all_gather(new_w_two.astype(jnp.bfloat16), "data", axis=1, tiled=True)
        h_last = run_stack(next_one_b, next_two_b, x_one.astype(jnp.float32))[0]
        loss_rows = jnp.sum(jnp.square(h_last - y_one.astype(jnp.float32)), axis=1) / (2 * d_model)
        return new_w_one, new_w_two, new_mom_one, new_mom_two, loss_rows, h_last

    return jax.shard_map(device_step, mesh=mesh, in_specs=(w_spec, w_spec, w_spec, w_spec, row_spec, row_spec, row_spec, row_spec), out_specs=(w_spec, w_spec, w_spec, w_spec, P("data"), row_spec), check_vma=False)
```

profile of v0, /device:TPU:0, one launch (start us, length us, event | category | flops | bytes accessed | tf_op | source)
XLA Modules:
  0.0 3828.5 jit_solution(9375290088268600012)
XLA Ops:
  19.6 151.9 %all-gather.5.cloned.1.call-done = bf16[32,512,1024]{2,1,0:T(8,128)(2,1)} async-done(((bf16[32,64,1024]{2,1,0:T(8,128)(2,1)}), bf16[32,512,1024]{2,1,0:T(8,128)(2,1)}) %all-gather.5.cloned.1.call-update) | async-done | bytes 33554448 | tf_op jit(solution)/shard_map/all_gather | solution.py:40
  177.3 151.9 %all-gather.7.cloned.1.call-done = bf16[32,1024,512]{2,1,0:T(8,128)(2,1)} async-done(((bf16[32,128,512]{2,1,0:T(8,128)(2,1)}), bf16[32,1024,512]{2,1,0:T(8,128)(2,1)}) %all-gather.7.cloned.1.call-update) | async-done | bytes 33554448 | tf_op jit(solution)/shard_map/all_gather | solution.py:41
  1692.9 28.7 reduce-scatter.223.cloned.1.call-done
  1723.5 28.9 reduce-scatter.225.cloned.1.call-done
  1784.7 28.9 reduce-scatter.229.cloned.1.call-done
  1815.4 28.9 reduce-scatter.231.cloned.1.call-done
  1846.1 28.9 reduce-scatter.233.cloned.1.call-done
  1907.3 28.9 reduce-scatter.237.cloned.1.call-done
  1938.0 28.8 reduce-scatter.239.cloned.1.call-done
  1999.1 28.9 reduce-scatter.243.cloned.1.call-done
  2029.7 28.9 reduce-scatter.245.cloned.1.call-done
  2091.0 28.9 reduce-scatter.249.cloned.1.call-done
  2121.7 28.9 reduce-scatter.251.cloned.1.call-done
  2182.9 28.9 reduce-scatter.255.cloned.1.call-done
  2274.6 29.5 reduce-scatter.133.cloned.1.call-done
  2305.7 29.7 reduce-scatter.135.cloned.1.call-done
  2336.9 29.5 reduce-scatter.137.cloned.1.call-done
  2368.0 29.1 reduce-scatter.139.cloned.1.call-done
  2398.7 29.1 reduce-scatter.141.cloned.1.call-done
  2429.4 29.1 reduce-scatter.143.cloned.1.call-done
  2460.1 29.0 reduce-scatter.145.cloned.1.call-done
  2490.6 29.1 reduce-scatter.147.cloned.1.call-done
  2521.3 29.0 reduce-scatter.149.cloned.1.call-done
  2551.9 29.0 reduce-scatter.151.cloned.1.call-done
  2582.4 29.0 reduce-scatter.153.cloned.1.call-done
  2612.9 29.0 reduce-scatter.155.cloned.1.call-done
  2643.5 29.0 reduce-scatter.157.cloned.1.call-done
  2674.0 29.1 reduce-scatter.159.cloned.1.call-done
  2704.7 29.0 reduce-scatter.161.cloned.1.call-done
  2735.2 29.1 reduce-scatter.163.cloned.1.call-done
  2765.9 29.0 reduce-scatter.165.cloned.1.call-done
  2796.5 29.1 reduce-scatter.167.cloned.1.call-done
  2827.2 29.1 reduce-scatter.169.cloned.1.call-done
  2857.8 29.1 reduce-scatter.171.cloned.1.call-done
  2888.5 29.1 reduce-scatter.173.cloned.1.call-done
  2919.2 29.0 reduce-scatter.175.cloned.1.call-done
  2949.8 29.0 reduce-scatter.177.cloned.1.call-done
  2980.3 29.2 reduce-scatter.179.cloned.1.call-done
  3011.0 29.1 reduce-scatter.181.cloned.1.call-done
  3041.7 29.2 reduce-scatter.183.cloned.1.call-done
  3072.4 29.0 reduce-scatter.185.cloned.1.call-done
  3103.0 29.0 reduce-scatter.187.cloned.1.call-done
  3133.6 29.1 reduce-scatter.189.cloned.1.call-done
  3164.3 29.0 reduce-scatter.191.cloned.1.call-done
  3236.7 113.5 %all-gather.9.cloned.1.call-done = bf16[32,512,1024]{2,0,1:T(8,128)(2,1)} async-done(((bf16[32,64,1024]{2,0,1:T(8,128)(2,1)}), bf16[32,512,1024]{2,0,1:T(8,128)(2,1)}) %all-gather.9.cloned.1.call-update) | async-done | bytes 33554448 | tf_op jit(solution)/shard_map/all_gather | solution.py:56
  3350.2 48.3 %fusion.872 = (bf16[1,512,1024]{2,0,1:T(2,128)(2,1)}, bf16[1,512,1024]{2,0,1:T(2,128)(2,1)}, bf16[1,512,1024]{2,0,1:T(2,128)(2,1)}, bf16[1,512,1024]{2,0,1:T(2,1...) fusion(bf16[32,512,1024]{2,0,1:T(8,128)(2,1)} %all-gather.9.clo, ...), kind=kLoop, calls=%fused_computation.1294 | loop fusion | bytes 27262976 | tf_op jit(solution)/shard_map/slice | solution.py:14
  3398.5 68.2 %fusion.871 = (bf16[1,512,1024]{2,0,1:T(2,128)(2,1)}, bf16[1,512,1024]{2,0,1:T(2,128)(2,1)}, bf16[1,512,1024]{2,0,1:T(2,128)(2,1)}, bf16[1,512,1024]{2,0,1:T(2,1...) fusion(bf16[32,512,1024]{2,0,1:T(8,128)(2,1)} %all-gather.9.clo, ...), kind=kLoop, calls=%fused_computation.1293 | loop fusion | bytes 39845888 | tf_op jit(solution)/shard_map/slice | solution.py:14
  3466.6 40.6 %all-gather.11.cloned.1.call-done = bf16[32,1024,512]{2,1,0:T(8,128)(2,1)} async-done(((bf16[32,128,512]{2,1,0:T(8,128)(2,1)}), bf16[32,1024,512]{2,1,0:T(8,128)(2,1)}) %all-gather.11.cloned.1.call-update) | async-done | bytes 33554448 | tf_op jit(solution)/shard_map/all_gather | solution.py:57
  (668 shorter events, 2017.4 us)
Async XLA Ops:
  19.5 1627.4 %reduce-scatter.193.cloned.1.call-start = ((), (), s32[]{:S(2)}) async-start(), calls=%async_computation.100 | async-start | bytes 1179648
  1330.7 513.6 %reduce-scatter.231.cloned.1.call-start = ((), (), s32[]{:S(2)}) async-start(), calls=%async_computation.119 | async-start | bytes 1179648
  1335.5 539.4 %reduce-scatter.233.cloned.1.call-start = ((), (), s32[]{:S(2)}) async-start(), calls=%async_computation.120 | async-start | bytes 1179648
  1341.4 564.1 %reduce-scatter.235.cloned.1.call-start = ((), (), s32[]{:S(2)}) async-start(), calls=%async_computation.121 | async-start | bytes 1179648
  1346.2 590.0 %reduce-scatter.237.cloned.1.call-start = ((), (), s32[]{:S(2)}) async-start(), calls=%async_computation.122 | async-start | bytes 1179648
  1352.1 614.7 %reduce-scatter.239.cloned.1.call-start = ((), (), s32[]{:S(2)}) async-start(), calls=%async_computation.123 | async-start | bytes 1179648
  1356.8 640.4 %reduce-scatter.241.cloned.1.call-start = ((), (), s32[]{:S(2)}) async-start(), calls=%async_computation.124 | async-start | bytes 1179648
  1362.7 665.3 %reduce-scatter.243.cloned.1.call-start = ((), (), s32[]{:S(2)}) async-start(), calls=%async_computation.125 | async-start | bytes 1179648
  1367.6 691.0 %reduce-scatter.245.cloned.1.call-start = ((), (), s32[]{:S(2)}) async-start(), calls=%async_computation.126 | async-start | bytes 1179648
  1373.5 715.7 %reduce-scatter.247.cloned.1.call-start = ((), (), s32[]{:S(2)}) async-start(), calls=%async_computation.127 | async-start | bytes 1179648
  1378.2 741.6 %reduce-scatter.249.cloned.1.call-start = ((), (), s32[]{:S(2)}) async-start(), calls=%async_computation.128 | async-start | bytes 1179648
  1384.1 766.5 %reduce-scatter.251.cloned.1.call-start = ((), (), s32[]{:S(2)}) async-start(), calls=%async_computation.129 | async-start | bytes 1179648
  1388.9 792.2 %reduce-scatter.253.cloned.1.call-start = ((), (), s32[]{:S(2)}) async-start(), calls=%async_computation.130 | async-start | bytes 1179648
  1394.7 817.1 %reduce-scatter.255.cloned.1.call-start = ((), (), s32[]{:S(2)}) async-start(), calls=%async_computation.131 | async-start | bytes 1179648
  1399.5 851.8 %reduce-scatter.129.cloned.1.call-start = ((), (), s32[]{:S(2)}) async-start(), calls=%async_computation.66 | async-start | bytes 1179648 | tf_op jit(solution)/shard_map/reduce_scatter | solution.py:48
  1406.2 866.8 %reduce-scatter.131.cloned.1.call-start = ((), (), s32[]{:S(2)}) async-start(), calls=%async_computation.67 | async-start | bytes 1179648 | tf_op jit(solution)/shard_map/reduce_scatter | solution.py:48
  1413.9 890.2 %reduce-scatter.133.cloned.1.call-start = ((), (), s32[]{:S(2)}) async-start(), calls=%async_computation.68 | async-start | bytes 1179648 | tf_op jit(solution)/shard_map/reduce_scatter | solution.py:48
  1420.3 915.0 %reduce-scatter.135.cloned.1.call-start = ((), (), s32[]{:S(2)}) async-start(), calls=%async_computation.69 | async-start | bytes 1179648 | tf_op jit(solution)/shard_map/reduce_scatter | solution.py:48
  1427.8 938.7 %reduce-scatter.137.cloned.1.call-start = ((), (), s32[]{:S(2)}) async-start(), calls=%async_computation.70 | async-start | bytes 1179648 | tf_op jit(solution)/shard_map/reduce_scatter | solution.py:48
  1434.1 963.0 %reduce-scatter.139.cloned.1.call-start = ((), (), s32[]{:S(2)}) async-start(), calls=%async_computation.71 | async-start | bytes 1179648 | tf_op jit(solution)/shard_map/reduce_scatter | solution.py:48
  1441.6 986.3 %reduce-scatter.141.cloned.1.call-start = ((), (), s32[]{:S(2)}) async-start(), calls=%async_computation.72 | async-start | bytes 1179648 | tf_op jit(solution)/shard_map/reduce_scatter | solution.py:48
  1448.4 1010.1 %reduce-scatter.143.cloned.1.call-start = ((), (), s32[]{:S(2)}) async-start(), calls=%async_computation.73 | async-start | bytes 1179648 | tf_op jit(solution)/shard_map/reduce_scatter | solution.py:48
  1455.8 1033.2 %reduce-scatter.145.cloned.1.call-start = ((), (), s32[]{:S(2)}) async-start(), calls=%async_computation.74 | async-start | bytes 1179648 | tf_op jit(solution)/shard_map/reduce_scatter | solution.py:48
  1462.3 1057.5 %reduce-scatter.147.cloned.1.call-start = ((), (), s32[]{:S(2)}) async-start(), calls=%async_computation.75 | async-start | bytes 1179648 | tf_op jit(solution)/shard_map/reduce_scatter | solution.py:48
  1469.7 1080.6 %reduce-scatter.149.cloned.1.call-start = ((), (), s32[]{:S(2)}) async-start(), calls=%async_computation.76 | async-start | bytes 1179648 | tf_op jit(solution)/shard_map/reduce_scatter | solution.py:48
  1476.1 1104.7 %reduce-scatter.151.cloned.1.call-start = ((), (), s32[]{:S(2)}) async-start(), calls=%async_computation.77 | async-start | bytes 1179648 | tf_op jit(solution)/shard_map/reduce_scatter | solution.py:48
  1483.7 1127.7 %reduce-scatter.153.cloned.1.call-start = ((), (), s32[]{:S(2)}) async-start(), calls=%async_computation.78 | async-start | bytes 1179648 | tf_op jit(solution)/shard_map/reduce_scatter | solution.py:48
  1490.1 1151.8 %reduce-scatter.155.cloned.1.call-start = ((), (), s32[]{:S(2)}) async-start(), calls=%async_computation.79 | async-start | bytes 1179648 | tf_op jit(solution)/shard_map/reduce_scatter | solution.py:48
  1497.5 1174.9 %reduce-scatter.157.cloned.1.call-start = ((), (), s32[]{:S(2)}) async-start(), calls=%async_computation.80 | async-start | bytes 1179648 | tf_op jit(solution)/shard_map/reduce_scatter | solution.py:48
  1504.0 1199.2 %reduce-scatter.159.cloned.1.call-start = ((), (), s32[]{:S(2)}) async-start(), calls=%async_computation.81 | async-start | bytes 1179648 | tf_op jit(solution)/shard_map/reduce_scatter | solution.py:48
  1511.4 1222.3 %reduce-scatter.161.cloned.1.call-start = ((), (), s32[]{:S(2)}) async-start(), calls=%async_computation.82 | async-start | bytes 1179648 | tf_op jit(solution)/shard_map/reduce_scatter | solution.py:48
  1518.1 1246.3 %reduce-scatter.163.cloned.1.call-start = ((), (), s32[]{:S(2)}) async-start(), calls=%async_computation.83 | async-start | bytes 1179648 | tf_op jit(solution)/shard_map/reduce_scatter | solution.py:48
  1525.5 1269.4 %reduce-scatter.165.cloned.1.call-start = ((), (), s32[]{:S(2)}) async-start(), calls=%async_computation.84 | async-start | bytes 1179648 | tf_op jit(solution)/shard_map/reduce_scatter | solution.py:48
  1531.9 1293.7 %reduce-scatter.167.cloned.1.call-start = ((), (), s32[]{:S(2)}) async-start(), calls=%async_computation.85 | async-start | bytes 1179648 | tf_op jit(solution)/shard_map/reduce_scatter | solution.py:48
  1539.3 1316.9 %reduce-scatter.169.cloned.1.call-start = ((), (), s32[]{:S(2)}) async-start(), calls=%async_computation.86 | async-start | bytes 1179648 | tf_op jit(solution)/shard_map/reduce_scatter | solution.py:48
  1545.7 1341.2 %reduce-scatter.171.cloned.1.call-start = ((), (), s32[]{:S(2)}) async-start(), calls=%async_computation.87 | async-start | bytes 1179648 | tf_op jit(solution)/shard_map/reduce_scatter | solution.py:48
  1553.7 1363.9 %reduce-scatter.173.cloned.1.call-start = ((), (), s32[]{:S(2)}) async-start(), calls=%async_computation.88 | async-start | bytes 1179648 | tf_op jit(solution)/shard_map/reduce_scatter | solution.py:48
  1560.1 1388.1 %reduce-scatter.175.cloned.1.call-start = ((), (), s32[]{:S(2)}) async-start(), calls=%async_computation.89 | async-start | bytes 1179648 | tf_op jit(solution)/shard_map/reduce_scatter | solution.py:48
  1567.6 1411.2 %reduce-scatter.177.cloned.1.call-start = ((), (), s32[]{:S(2)}) async-start(), calls=%async_computation.90 | async-start | bytes 1179648 | tf_op jit(solution)/shard_map/reduce_scatter | solution.py:48
  1574.0 1435.5 %reduce-scatter.179.cloned.1.call-start = ((), (), s32[]{:S(2)}) async-start(), calls=%async_computation.91 | async-start | bytes 1179648 | tf_op jit(solution)/shard_map/reduce_scatter | solution.py:48
  1581.4 1458.7 %reduce-scatter.181.cloned.1.call-start = ((), (), s32[]{:S(2)}) async-start(), calls=%async_computation.92 | async-start | bytes 1179648 | tf_op jit(solution)/shard_map/reduce_scatter | solution.py:48
  1588.0 1482.9 %reduce-scatter.183.cloned.1.call-start = ((), (), s32[]{:S(2)}) async-start(), calls=%async_computation.93 | async-start | bytes 1179648 | tf_op jit(solution)/shard_map/reduce_scatter | solution.py:48
  1595.4 1506.0 %reduce-scatter.185.cloned.1.call-start = ((), (), s32[]{:S(2)}) async-start(), calls=%async_computation.94 | async-start | bytes 1179648 | tf_op jit(solution)/shard_map/reduce_scatter | solution.py:48
  1601.9 1530.1 %reduce-scatter.187.cloned.1.call-start = ((), (), s32[]{:S(2)}) async-start(), calls=%async_computation.95 | async-start | bytes 1179648 | tf_op jit(solution)/shard_map/reduce_scatter | solution.py:48
  1609.3 1553.4 %reduce-scatter.189.cloned.1.call-start = ((), (), s32[]{:S(2)}) async-start(), calls=%async_computation.96 | async-start | bytes 1179648 | tf_op jit(solution)/shard_map/reduce_scatter | solution.py:48
  1615.7 1577.6 %reduce-scatter.191.cloned.1.call-start = ((), (), s32[]{:S(2)}) async-start(), calls=%async_computation.97 | async-start | bytes 1179648 | tf_op jit(solution)/shard_map/reduce_scatter | solution.py:48
  1646.9 1703.3 %all-gather.9.cloned.1.call-start = ((), (), s32[]{:S(2)}) async-start(), calls=%async_computation.98 | async-start | bytes 37748736 | tf_op jit(solution)/shard_map/all_gather | solution.py:56
  2250.8 1256.5 %all-gather.11.cloned.1.call-start = ((), (), s32[]{:S(2)}) async-start(), calls=%async_computation.99 | async-start | bytes 37748736 | tf_op jit(solution)/shard_map/all_gather | solution.py:57
  (109 other events, 8419.3 us)
Sparse Core Ops, SparseCore 0:
  13.4 158.0 all-gather.4
  173.9 155.2 all-gather.6
  1234.5 27.5 reduce-scatter.192
  1265.6 27.5 reduce-scatter.194
  1296.2 27.5 reduce-scatter.196
  1326.7 27.5 reduce-scatter.198
  1388.1 27.5 reduce-scatter.202
  1418.9 27.5 reduce-scatter.204
  1480.1 27.5 reduce-scatter.208
  1510.7 27.5 reduce-scatter.210
  1541.4 27.5 reduce-scatter.212
  1602.5 27.5 reduce-scatter.216
  1694.1 27.5 reduce-scatter.222
  1786.0 27.5 reduce-scatter.228
  1816.7 27.5 reduce-scatter.230
  1847.4 27.5 reduce-scatter.232
  1877.9 27.5 reduce-scatter.234
  1939.1 27.5 reduce-scatter.238
  1969.7 27.5 reduce-scatter.240
  2000.4 27.5 reduce-scatter.242
  2031.1 27.5 reduce-scatter.244
  2092.3 27.5 reduce-scatter.248
  2123.0 27.5 reduce-scatter.250
  2153.5 27.5 reduce-scatter.252
  2184.2 27.5 reduce-scatter.254
  2245.4 27.5 reduce-scatter.130
  2338.9 27.5 reduce-scatter.136
  2369.6 27.5 reduce-scatter.138
  2431.0 27.5 reduce-scatter.142
  2461.5 27.5 reduce-scatter.144
  2492.2 27.5 reduce-scatter.146
  2522.7 27.5 reduce-scatter.148
  2553.2 27.5 reduce-scatter.150
  2706.1 27.5 reduce-scatter.160
  2736.8 27.5 reduce-scatter.162
  2767.3 27.5 reduce-scatter.164
  2828.7 27.5 reduce-scatter.168
  2859.4 27.5 reduce-scatter.170
  2920.6 27.5 reduce-scatter.174
  2981.8 27.5 reduce-scatter.178
  3012.5 27.5 reduce-scatter.180
  3043.3 27.5 reduce-scatter.182
  3073.8 27.5 reduce-scatter.184
  3104.4 27.5 reduce-scatter.186
  3135.1 27.5 reduce-scatter.188
  3165.7 27.5 reduce-scatter.190
  3194.9 155.2 all-gather.8
  3352.0 155.2 all-gather.10
  (20 shorter events, 549.7 us)
where the time goes:
time: 3840 us; the launch traced here: 3830 us
  waiting for transfers between devices  1860 us (48%)
  matrix products  1540 us (40%)
  local copies, waits for them, and re-layouts  351 us (9%)
  other arithmetic  53.2 us (1%)
    reduce_scatter x32, waiting for transfers between devices, device_step(): lax.psum_scatter(grad_out, 'data', scatter_dimension=0, tiled=True)  893 us
    dot_general x64, matrix products, run_stack(): jnp.dot(hidden, w_two_b[layer_idx], preferred_element_type=jnp.float32)  518 us
    unnamed x100, waiting for transfers between devices  510 us
    dot_general x31, matrix products, layer_grads(): jnp.einsum('td,fd->tf', d_low, w_out, preferred_element_type=jnp.float32)  285 us
    unnamed x280, local copies, waits for them, and re-layouts  222 us
    dot_general x32, matrix products, layer_grads(): jnp.einsum('tf,td->fd', hidden, d_low, preferred_element_type=jnp.float32)  218 us
    dot_general x31, matrix products, device_step(): jnp.einsum('tf,df->td', d_pre, w_one_b[layer_idx], preferred_element_type...  199 us
    dot_general x32, matrix products, layer_grads(): jnp.einsum('td,tf->df', act_in, d_pre, preferred_element_type=jnp.float32)  173 us
  transfers between devices with their start and end apart: 68, of which 53 were waited for; matrix products, arithmetic and copies ran while one was open for 19% of the time, Pallas kernels for 0%

commit v1 on v0

v1 whole, which is shorter than its diff:
```python
import functools

import jax
import jax.numpy as jnp
from jax import lax
from jax.experimental import pallas as pl
from jax.experimental.pallas import tpu as pltpu
from jax.sharding import PartitionSpec as P

LEARN_RATE = 0.1
MOMENTUM = 0.9
GELU_C = 0.7978845608028654
GELU_K = 0.044715
MESH = pl.DeviceIdType.MESH
F32 = jnp.float32
BF16 = jnp.bfloat16
LAG = 2
SLOTS = 4 * LAG + 1
ANY = pl.BlockSpec(memory_space=pl.ANY)


def place():
    me = lax.axis_index("data")
    core, col, row = me % 2, (me // 2) % 2, me // 4
    return me, core, col, row


def index_of(row, col, core):
    return 4 * row + 2 * col + core


def greet(peers):
    barrier = pltpu.get_barrier_semaphore()
    for peer in peers:
        pl.semaphore_signal(barrier, inc=1, device_id=(peer,), device_id_type=MESH)
    pl.semaphore_wait(barrier, len(peers))


def forward_kernel(train, layers, tile, scale, *refs):
    if train:
        (w1s, w2s, x_in, y_in, d_out, zt_out, at_out, p_out, w1t_out, w2t_out,
         w1, w2, h, xb, send_sem, recv_sem, own_sem, io_sem,
         zt_st, at_st, p_st, w1t_st, w2t_st, st_sem, wt_sem) = refs
    else:
        (w1s, w2s, x_in, h_out, w1, w2, h, xb, send_sem, recv_sem, own_sem, io_sem) = refs
    me, core, col, row = place()
    j_p = index_of(row, col, 1 - core)
    j_x = index_of(row, 1 - col, core)
    j_y = index_of(1 - row, col, core)
    j_d = index_of(1 - row, 1 - col, core)
    p_x = index_of(row, 1 - col, 1 - core)
    p_y = index_of(1 - row, col, 1 - core)
    p_d = index_of(1 - row, 1 - col, 1 - core)
    r1, r2 = w1s.shape[1], w2s.shape[1]
    rows = h.shape[0]
    tiles = rows // tile

    greet((j_p, j_x, j_y))

    def part(which, slot, j):
        if which == 1:
            return w1.at[slot, pl.ds(pl.multiple_of(j * r1, r1), r1)]
        return w2.at[slot, pl.ds(pl.multiple_of(j * r2, r2), r2)]

    sends = (
        (1, me, j_y, j_y), (1, me, j_x, j_x), (1, me, j_p, j_p),
        (2, me, j_x, j_x), (2, me, j_y, j_y), (2, me, j_p, j_p),
        (1, j_y, j_x, j_d), (1, j_y, j_p, p_y), (2, j_x, j_y, j_d), (2, j_x, j_p, p_x),
        (1, j_x, j_p, p_x), (2, j_y, j_p, p_y),
        (1, j_d, j_p, p_d), (2, j_d, j_p, p_d),
    )

    def channel(layer, k, incoming=False):
        slot = layer % SLOTS
        which, out, to, inc = sends[k]
        ref = part(which, slot, inc if incoming else out)
        return pltpu.make_async_remote_copy(
            src_ref=ref, dst_ref=ref, send_sem=send_sem.at[slot, k], recv_sem=recv_sem.at[slot, k],
            device_id=(to,), device_id_type=MESH)

    def start(layer, ks):
        for k in ks:
            channel(layer, k).start()

    def arrive(layer, ks):
        for k in ks:
            channel(layer, k, True).wait_recv()

    def own(layer):
        slot = layer % SLOTS
        return (pltpu.make_async_copy(w1s.at[layer], part(1, slot, me), own_sem.at[slot, 0]),
                pltpu.make_async_copy(w2s.at[layer], part(2, slot, me), own_sem.at[slot, 1]))

    def gather(i):
        def on(layer):
            return jnp.logical_and(layer >= 0, layer < layers)

        @pl.when(on(i))
        def _():
            arrive(i, (2, 5, 7, 9, 10, 11, 12, 13))

        @pl.when(on(i + LAG))
        def _():
            arrive(i + LAG, (6, 8))
            start(i + LAG, (12, 13))

        @pl.when(on(i + 2 * LAG))
        def _():
            arrive(i + 2 * LAG, (0, 1, 3, 4))
            start(i + 2 * LAG, (6, 8, 7, 9, 10, 11))

        @pl.when(on(i + 3 * LAG))
        def _():
            for copy in own(i + 3 * LAG):
                copy.wait()
            start(i + 3 * LAG, (0, 3, 1, 4, 2, 5))

        @pl.when(on(i + 3 * LAG + 1))
        def _():
            for copy in own(i + 3 * LAG + 1):
                copy.start()

    def saved(layer, t, st):
        cols = pl.ds(pl.multiple_of(t * tile, tile), tile)
        return (pltpu.make_async_copy(zt_st.at[st], zt_out.at[layer, :, cols], st_sem.at[st, 0]),
                pltpu.make_async_copy(at_st.at[st], at_out.at[layer, :, cols], st_sem.at[st, 1]),
                pltpu.make_async_copy(p_st.at[st], p_out.at[layer, cols], st_sem.at[st, 2]))

    def turned(layer):
        return (pltpu.make_async_copy(w1t_st, w1t_out.at[layer], wt_sem.at[0]),
                pltpu.make_async_copy(w2t_st, w2t_out.at[layer], wt_sem.at[1]))

    def compute(layer):
        slot = layer % SLOTS

        def one(t, _):
            where = pl.ds(pl.multiple_of(t * tile, tile), tile)
            h_val = h[where, :]
            a_val = h_val.astype(BF16)
            u = jnp.dot(a_val, w1[slot], preferred_element_type=F32)
            sq = u * u
            w = 0.5 * (1.0 + jnp.tanh(u * (GELU_C + (GELU_C * GELU_K) * sq)))
            z = u * w
            z_low = z.astype(BF16)
            if train:
                step = layer * tiles + t
                st = step % 2

                @pl.when(step >= 2)
                def _():
                    for copy in saved((step - 2) // tiles, (step - 2) % tiles, st):
                        copy.wait()

                p_st[st] = w + (z * (1.0 - w)) * (2.0 * GELU_C + (6.0 * GELU_C * GELU_K) * sq)
                zt_st[st] = z_low.T
                at_st[st] = a_val.T
                for copy in saved(layer, t, st):
                    copy.start()
            h[where, :] = h_val + jnp.dot(z_low, w2[slot], preferred_element_type=F32)
            return 0

        lax.fori_loop(0, tiles, one, 0)
        if train:
            @pl.when(layer >= 1)
            def _():
                for copy in turned(layer - 1):
                    copy.wait()

            w1t_st[...] = w1[slot].T
            w2t_st[...] = w2[slot].T
            for copy in turned(layer):
                copy.start()

    x_copy = pltpu.make_async_copy(x_in, xb, io_sem.at[0])
    x_copy.start()
    for copy in own(0):
        copy.start()
    x_copy.wait()

    def widen(t, _):
        where = pl.ds(pl.multiple_of(t * 256, 256), 256)
        h[where, :] = xb[where, :].astype(F32)
        return 0

    lax.fori_loop(0, rows // 256, widen, 0)

    def turn(n, _):
        i = n - 3 * LAG
        gather(i)

        @pl.when(i >= 0)
        def _():
            compute(i)
            for k in range(len(sends)):
                channel(i, k).wait_send()

        return 0

    lax.fori_loop(0, layers + 3 * LAG, turn, 0)

    if train:
        last = layers * tiles
        for step in (last - 2, last - 1):
            for copy in saved(step // tiles, step % tiles, step % 2):
                copy.wait()
        for copy in turned(layers - 1):
            copy.wait()
        y_copy = pltpu.make_async_copy(y_in, xb, io_sem.at[0])
        y_copy.start()
        y_copy.wait()

        def close(t, _):
            where = pl.ds(pl.multiple_of(t * 256, 256), 256)
            h[where, :] = (h[where, :] - xb[where, :].astype(F32)) / scale
            return 0

        lax.fori_loop(0, rows // 256, close, 0)
    out_copy = pltpu.make_async_copy(h, d_out if train else h_out, io_sem.at[1])
    out_copy.start()
    out_copy.wait()


def forward(train, w1s, w2s, x, y=None, scale=None, tile=512, cid=0):
    layers, r1, d_ff = w1s.shape
    r2, d_model = w2s.shape[1:]
    rows = x.shape[0]
    sds = jax.ShapeDtypeStruct
    h_shape = sds((rows, d_model), F32)
    scratch = [
        pltpu.VMEM((SLOTS, d_model, d_ff), BF16), pltpu.VMEM((SLOTS, d_ff, d_model), BF16),
        pltpu.VMEM((rows, d_model), F32), pltpu.VMEM((rows, d_model), BF16),
        pltpu.SemaphoreType.DMA((SLOTS, 14)), pltpu.SemaphoreType.DMA((SLOTS, 14)),
        pltpu.SemaphoreType.DMA((SLOTS, 2)), pltpu.SemaphoreType.DMA((2,)),
    ]
    out = h_shape
    args = (w1s, w2s, x)
    if train:
        out = (h_shape, sds((layers, d_ff, rows), BF16), sds((layers, d_model, rows), BF16),
               sds((layers, rows, d_ff), F32), sds((layers, d_ff, d_model), BF16), sds((layers, d_model, d_ff), BF16))
        args = (w1s, w2s, x, y)
        scratch += [
            pltpu.VMEM((2, d_ff, tile), BF16), pltpu.VMEM((2, d_model, tile), BF16), pltpu.VMEM((2, tile, d_ff), F32),
            pltpu.VMEM((d_ff, d_model), BF16), pltpu.VMEM((d_model, d_ff), BF16),
            pltpu.SemaphoreType.DMA((2, 3)), pltpu.SemaphoreType.DMA((2,)),
        ]
    return pl.pallas_call(
        functools.partial(forward_kernel, train, layers, tile, scale),
        out_shape=out,
        in_specs=[ANY] * len(args),
        out_specs=jax.tree.map(lambda _: ANY, out),
        scratch_shapes=scratch,
        compiler_params=pltpu.CompilerParams(collective_id=cid, has_side_effects=True, vmem_limit_bytes=60 * 2**20),
        name="fwd_train" if train else "fwd_eval",
    )(*args)


WAIT_D, WAIT_1, WAIT_2 = 1, 2, 2


def backward_kernel(layers, tile, *refs):
    (d_in, zt_in, at_in, p_in, w1t_in, w2t_in, g1_out, g2_out,
     d, db, r, zt, at, p, w1t, w2t, ga, gb, da, dbuf, sa, sb, ra, rb, ta, tb, fa, fb, oa, ob,
     in_sem, d_sem, xd_send, xd_recv, x1_send, x1_recv, x2_send, x2_recv, out_sem) = refs
    me, core, col, row = place()
    j_p = index_of(row, col, 1 - core)
    j_x = index_of(row, 1 - col, core)
    j_y = index_of(1 - row, col, core)
    rows = d.shape[0]
    tiles = rows // tile
    n_g, n_r1, n_s, n_r2, n_t = 2, 2 * WAIT_1, WAIT_1 + 1, 2 * WAIT_2, WAIT_2 + 1
    n_d = 2 * WAIT_D
    s1, s2 = ga.shape[4], gb.shape[4]

    greet((j_p, j_x, j_y))

    def loads(n):
        layer, s = layers - 1 - n, n % 2
        return tuple(
            pltpu.make_async_copy(src.at[layer], dst.at[s], in_sem.at[s, k])
            for k, (src, dst) in enumerate(((w2t_in, w2t), (p_in, p), (w1t_in, w1t), (zt_in, zt), (at_in, at))))

    def remote(src, dst, send, recv, to):
        return pltpu.make_async_remote_copy(
            src_ref=src, dst_ref=dst, send_sem=send, recv_sem=recv, device_id=(to,), device_id_type=MESH)

    def hop_d(n):
        g, s = n % n_g, n % n_d
        return (remote(ga.at[g, 1 - core], da.at[s], xd_send.at[s, 0], xd_recv.at[s, 0], j_p),
                remote(gb.at[g, 1 - core], dbuf.at[s], xd_send.at[s, 1], xd_recv.at[s, 1], j_p))

    def hop_1(n):
        g, s = n % n_s, n % n_r1
        return (remote(sa.at[g, 1 - row], ra.at[s], x1_send.at[s, 0], x1_recv.at[s, 0], j_y),
                remote(sb.at[g, 1 - col], rb.at[s], x1_send.at[s, 1], x1_recv.at[s, 1], j_x))

    def hop_2(n):
        g, s = n % n_t, n % n_r2
        return (remote(ta.at[g, 1 - col], fa.at[s], x2_send.at[s, 0], x2_recv.at[s, 0], j_x),
                remote(tb.at[g, 1 - row], fb.at[s], x2_send.at[s, 1], x2_recv.at[s, 1], j_y))

    def results(n):
        layer, s = layers - 1 - n, n % 2
        return (pltpu.make_async_copy(oa.at[s], g1_out.at[layer], out_sem.at[s, 0]),
                pltpu.make_async_copy(ob.at[s], g2_out.at[layer], out_sem.at[s, 1]))

    def on(n):
        return jnp.logical_and(n >= 0, n < layers)

    def add(x, y):
        return (x.astype(F32) + y.astype(F32)).astype(BF16)

    lag_2 = 1 + WAIT_D
    lag_3 = lag_2 + WAIT_1
    lag_4 = lag_3 + WAIT_2

    def exchange(n):
        @pl.when(on(n - lag_4))
        def _():
            m = n - lag_4

            @pl.when(m >= 2)
            def _():
                for copy in results(m - 2):
                    copy.wait()

            for copy in hop_2(m):
                copy.wait()
            oa[m % 2] = add(ta[m % n_t, col], fa[m % n_r2])
            ob[m % 2] = add(tb[m % n_t, row], fb[m % n_r2])
            for copy in results(m):
                copy.start()

        @pl.when(on(n - lag_3))
        def _():
            m = n - lag_3
            for copy in hop_1(m):
                copy.wait()
            ta[m % n_t] = add(sa[m % n_s, row], ra[m % n_r1])
            tb[m % n_t] = add(sb[m % n_s, col], rb[m % n_r1])
            for copy in hop_2(m):
                copy.start()

        @pl.when(on(n - lag_2))
        def _():
            m = n - lag_2
            for copy in hop_d(m):
                copy.wait()
            sa[m % n_s] = add(ga[m % n_g, core], da[m % n_d])
            sb[m % n_s] = add(gb[m % n_g, core], dbuf[m % n_d])
            for copy in hop_1(m):
                copy.start()

        @pl.when(on(n - 1))
        def _():
            for copy in hop_d(n - 1):
                copy.start()

    def compute(n):
        s, g = n % 2, n % n_g

        def one(t, _):
            where = pl.ds(pl.multiple_of(t * tile, tile), tile)
            d_val = d[where, :]
            d_low = d_val.astype(BF16)
            db[where, :] = d_low
            q = jnp.dot(d_low, w2t[s], preferred_element_type=F32)
            r_val = (p[s, where, :] * q).astype(BF16)
            r[where, :] = r_val

            @pl.when(n < layers - 1)
            def _():
                d[where, :] = d_val + jnp.dot(r_val, w1t[s], preferred_element_type=F32)

            return 0

        lax.fori_loop(0, tiles, one, 0)

        def out_grad(m, _):
            val = jnp.dot(zt[s, pl.ds(pl.multiple_of(m * 4 * s2, 4 * s2), 4 * s2), :], db[...], preferred_element_type=F32)
            val = val.astype(BF16)
            for k in range(4):
                gb[g, k % 2, k // 2, m] = val[k * s2:(k + 1) * s2]
            return 0

        def in_grad(m, _):
            val = jnp.dot(at[s, pl.ds(pl.multiple_of(m * 4 * s1, 4 * s1), 4 * s1), :], r[...], preferred_element_type=F32)
            val = val.astype(BF16)
            for k in range(4):
                ga[g, k % 2, m, k // 2] = val[k * s1:(k + 1) * s1]
            return 0

        lax.fori_loop(0, 2, out_grad, 0)
        lax.fori_loop(0, 2, in_grad, 0)

    d_copy = pltpu.make_async_copy(d_in, d, d_sem)
    d_copy.start()
    for copy in loads(0):
        copy.start()
    d_copy.wait()

    def turn(n, _):
        exchange(n)

        @pl.when(n < layers)
        def _():
            for copy in loads(n):
                copy.wait()

            @pl.when(n + 1 < layers)
            def _():
                for copy in loads(n + 1):
                    copy.start()

            compute(n)

        return 0

    lax.fori_loop(0, layers + lag_4, turn, 0)
    for n in (layers - 2, layers - 1):
        for copy in results(n):
            copy.wait()


def backward(d0, zt, at, p, w1t, w2t, n_dev, tile=512, cid=1):
    layers, d_ff, rows = zt.shape
    d_model = d0.shape[1]
    s1, s2 = d_model // n_dev, d_ff // n_dev
    sds = jax.ShapeDtypeStruct
    vm, sem = pltpu.VMEM, pltpu.SemaphoreType.DMA
    n_g, n_d, n_r1, n_s, n_r2, n_t = 2, 2 * WAIT_D, 2 * WAIT_1, WAIT_1 + 1, 2 * WAIT_2, WAIT_2 + 1
    scratch = [
        vm((rows, d_model), F32), vm((rows, d_model), BF16), vm((rows, d_ff), BF16),
        vm((2, d_ff, rows), BF16), vm((2, d_model, rows), BF16), vm((2, rows, d_ff), F32),
        vm((2, d_ff, d_model), BF16), vm((2, d_model, d_ff), BF16),
        vm((n_g, 2, 2, 2, s1, d_ff), BF16), vm((n_g, 2, 2, 2, s2, d_model), BF16),
        vm((n_d, 2, 2, s1, d_ff), BF16), vm((n_d, 2, 2, s2, d_model), BF16),
        vm((n_s, 2, 2, s1, d_ff), BF16), vm((n_s, 2, 2, s2, d_model), BF16),
        vm((n_r1, 2, s1, d_ff), BF16), vm((n_r1, 2, s2, d_model), BF16),
        vm((n_t, 2, s1, d_ff), BF16), vm((n_t, 2, s2, d_model), BF16),
        vm((n_r2, s1, d_ff), BF16), vm((n_r2, s2, d_model), BF16),
        vm((2, s1, d_ff), BF16), vm((2, s2, d_model), BF16),
        sem((2, 5)), sem(()), sem((n_d, 2)), sem((n_d, 2)), sem((n_r1, 2)), sem((n_r1, 2)),
        sem((n_r2, 2)), sem((n_r2, 2)), sem((2, 2)),
    ]
    return pl.pallas_call(
        functools.partial(backward_kernel, layers, tile),
        out_shape=(sds((layers, s1, d_ff), BF16), sds((layers, s2, d_model), BF16)),
        in_specs=[ANY] * 6,
        out_specs=(ANY, ANY),
        scratch_shapes=scratch,
        compiler_params=pltpu.CompilerParams(collective_id=cid, has_side_effects=True, vmem_limit_bytes=63 * 2**20),
        name="bwd",
    )(d0, zt, at, p, w1t, w2t)


def solution(mesh):
    n_dev = mesh.shape["data"]
    w_spec = P(None, "data", None)
    row_spec = P("data", None)

    def device_step(w_one, w_two, mom_one, mom_two, x_zero, y_zero, x_one, y_one):
        tok_dev, d_model = x_zero.shape
        scale = float(n_dev * tok_dev * d_model)
        d0, zt, at, p, w1t, w2t = forward(True, w_one.astype(BF16), w_two.astype(BF16), x_zero, y_zero, scale, cid=0)
        g1, g2 = backward(d0, zt, at, p, w1t, w2t, n_dev, cid=1)
        new_mom_one = MOMENTUM * mom_one + g1.astype(F32)
        new_mom_two = MOMENTUM * mom_two + g2.astype(F32)
        new_w_one = w_one - LEARN_RATE * new_mom_one
        new_w_two = w_two - LEARN_RATE * new_mom_two
        h_last = forward(False, new_w_one.astype(BF16), new_w_two.astype(BF16), x_one, cid=2)
        loss_rows = jnp.sum(jnp.square(h_last - y_one.astype(F32)), axis=1) / (2 * d_model)
        return new_w_one, new_w_two, new_mom_one, new_mom_two, loss_rows, h_last

    return jax.shard_map(device_step, mesh=mesh, in_specs=(w_spec, w_spec, w_spec, w_spec, row_spec, row_spec, row_spec, row_spec), out_specs=(w_spec, w_spec, w_spec, w_spec, P("data"), row_spec), check_vma=False)
```

time: 3840 us -> 982 us (0.26)
  waiting for transfers between devices: 1860 us -> 0 us
  matrix products: 1540 us -> 0 us
  Pallas kernels: 0 us -> 939 us
  local copies, waits for them, and re-layouts: 351 us -> 4.67 us
    dot_general x222 -> x0, matrix products: 1540 us -> none  [the longest x64 518 us: run_stack(): jnp.dot(hidden, w_two_b[layer_idx], preferred_element_type=jnp.float32)]
    pallas_call x0 -> x3, Pallas kernels: none -> 939 us  [the longest x2 630 us: forward(): pl.pallas_call(functools.partial(forward_kernel, train, layers, tile, sca...]
    reduce_scatter x32 -> x0, waiting for transfers between devices: 893 us -> none  [device_step(): lax.psum_scatter(grad_out, 'data', scatter_dimension=0, tiled=True)]
    unnamed x100 -> x0, waiting for transfers between devices: 510 us -> none
    all_gather x4 -> x0, waiting for transfers between devices: 458 us -> none  [the longest x1 152 us: device_step(): lax.all_gather(w_one.astype(jnp.bfloat16), 'data', axis=1, tiled=True)]
    unnamed x280 -> x7, local copies, waits for them, and re-layouts: 222 us -> 4.67 us
    slice x2 -> x0, local copies, waits for them, and re-layouts: 116 us -> none  [run_stack(): w_one_b[layer_idx]]
  transfers between devices with their start and end apart: 68 -> 0, of which waited for: 53 -> 0; matrix products, arithmetic and copies ran while one was open for 19% -> 0% of each run, Pallas kernels for 0% -> 0%
where the time goes in v1:
time: 982 us
  Pallas kernels  939 us (96%)
  other arithmetic  38.1 us (4%)
    pallas_call x2, Pallas kernels, forward(): pl.pallas_call(functools.partial(forward_kernel, train, layers, tile, sca...  630 us
    pallas_call x1, Pallas kernels, backward(): pl.pallas_call(functools.partial(backward_kernel, layers, tile), out_shap...  309 us

profile of v1, /device:TPU:0, one launch (start us, length us, event | category | flops | bytes accessed | tf_op | source)
XLA Modules:
  0.0 982.1 jit_solution(15945272282132511969)
XLA Ops:
  0.6 0.0 copy-start
  0.6 6.3 convert_element_type.21.refs_0_
  6.9 0.8 copy-done
  7.7 2.6 convert_element_type.22.refs_1_
  10.4 335.9 %fwd_train.1 = (f32[1536,512]{1,0:T(8,128)}, bf16[32,1024,1536]{2,1,0:T(8,128)(2,1)}, bf16[32,512,1536]{2,1,0:T(8,128)(2,1)}, f32[32,1536,1024]{2,1,0:T(8,128)},...) custom-call(bf16[32,64,1024]{2,1,0:T(8,128)(2,1)} %convert_element_type.21.refs_0_, ...), custom_call_target="tpu_custom_call" | custom-call | tf_op jit(solution)/shard_map/fwd_train/pallas_call | solution.py:246
  346.3 308.6 %bwd.1 = (bf16[32,64,1024]{2,1,0:T(8,128)(2,1)}, bf16[32,128,512]{2,1,0:T(8,128)(2,1)}) custom-call(f32[1536,512]{1,0:T(8,128)} %get-tuple-element.14.refs_0_, bf16[32,1024,1536]{2,1,0:T(8,128)(2,1)} %get-tuple-element.15.refs_1_, bf16[32,512,1536]{2,1,0:T(8,128)(2,1)} %get-tuple-element.16.refs_2_, f32[32,1536,1024]{2,1,0:T(8,128)} %get-tuple-element.17.refs_3_, ...), custom_call_target="tpu_custom_call" | custom-call | tf_op jit(solution)/shard_map/bwd/pallas_call | solution.py:445
  654.8 0.0 copy-start.1
  654.8 13.9 %fusion.1 = (bf16[32,64,1024]{2,1,0:T(8,128)(2,1)}, f32[32,64,1024]{2,1,0:T(8,128)}, f32[32,64,1024]{2,1,0:T(8,128)}) fusion(f32[32,64,1024]{2,1,0:T(8,128)} %param.8, bf16[32,64,1024]{2,1,0:T(8,128)(2,1)} %get-tuple-element.20, f32[32,64,1024]{2,1,0:T(8,128)} %param.10), kind=kLoop, calls=%fused_computation.7 | loop fusion | flops 12582912 | bytes 41943040 | tf_op jit(solution)/shard_map/convert_element_type | solution.py:470
  668.7 0.0 copy-done.1
  668.7 12.4 %fusion = (bf16[32,128,512]{2,1,0:T(8,128)(2,1)}, f32[32,128,512]{2,1,0:T(8,128)}, f32[32,128,512]{2,1,0:T(8,128)}) fusion(f32[32,128,512]{2,1,0:T(8,128)} %param.9, bf16[32,128,512]{2,1,0:T(8,128)(2,1)S(1)} %copy-done.1, f32[32,128,512]{2,1,0:T(8,128)} %param.11), kind=kLoop, calls=%fused_computation.6 | loop fusion | flops 12582912 | bytes 41943040 | tf_op jit(solution)/shard_map/convert_element_type | solution.py:470
  681.1 0.0 copy-start.2
  681.1 294.2 %fwd_eval.1 = f32[1536,512]{1,0:T(8,128)} custom-call(bf16[32,64,1024]{2,1,0:T(8,128)(2,1)} %get-tuple-element.25.refs_0_, bf16[32,128,512]{2,1,0:T(8,128)(2,1)} %get-tuple-element.22.refs_1_, bf16[1536,512]{1,0:T(8,128)(2,1)} %refs_2_.3), custom_call_target="tpu_custom_call" | custom-call | tf_op jit(solution)/shard_map/fwd_eval/pallas_call | solution.py:246
  975.3 0.0 copy-done.2
  975.3 2.4 multiply_reduce_fusion
  977.6 0.6 broadcast_multiply_fusion
  978.2 3.9 copy.15
Async XLA Ops:
  0.6 7.1 copy-start
  654.8 13.9 %copy-start.1 = (bf16[32,128,512]{2,1,0:T(8,128)(2,1)S(1)}, bf16[32,128,512]{2,1,0:T(8,128)(2,1)}, u32[]{:S(2)}) copy-start(bf16[32,128,512]{2,1,0:T(8,128)(2,1)} %get-tuple-element.21) | copy-start | bytes 12582916
  681.1 294.2 %copy-start.2 = (bf16[1536,512]{1,0:T(8,128)(2,1)S(1)}, bf16[1536,512]{1,0:T(8,128)(2,1)}, u32[]{:S(2)}) copy-start(bf16[1536,512]{1,0:T(8,128)(2,1)} %param.15) | copy-start | bytes 4718596

commit v2 on v1

v2 whole, which is shorter than its diff:
```python
import functools

import jax
import jax.numpy as jnp
from jax import lax
from jax.experimental import pallas as pl
from jax.experimental.pallas import tpu as pltpu
from jax.sharding import PartitionSpec as P

LEARN_RATE = 0.1
MOMENTUM = 0.9
GELU_C = 0.7978845608028654
GELU_K = 0.044715
MESH = pl.DeviceIdType.MESH
F32 = jnp.float32
BF16 = jnp.bfloat16
AHEAD_CORE, AHEAD_RELAY, AHEAD_OWN = 1, 2, 4
SLOTS = AHEAD_OWN + 2
CHUNK = 512
ANY = pl.BlockSpec(memory_space=pl.ANY)


def place():
    me = lax.axis_index("data")
    core, col, row = me % 2, (me // 2) % 2, me // 4
    return me, core, col, row


def index_of(row, col, core):
    return 4 * row + 2 * col + core


def greet(peers):
    barrier = pltpu.get_barrier_semaphore()
    for peer in peers:
        pl.semaphore_signal(barrier, inc=1, device_id=(peer,), device_id_type=MESH)
    pl.semaphore_wait(barrier, len(peers))


def forward_kernel(train, layers, tile, scale, *refs):
    if train:
        (w1s, w2s, x_in, y_in, d_out, zt_out, at_out, p_out, w1t_out, w2t_out,
         w1, w2, h, xb, s1_st, s2_st, send_sem, recv_sem, own_sem, io_sem,
         zt_st, at_st, p_st, w1t_st, w2t_st, st_sem, wt_sem) = refs
    else:
        (w1s, w2s, x_in, h_out, w1, w2, h, xb, s1_st, s2_st, send_sem, recv_sem, own_sem, io_sem) = refs
    me, core, col, row = place()
    j_p = index_of(row, col, 1 - core)
    j_x = index_of(row, 1 - col, core)
    j_y = index_of(1 - row, col, core)
    j_d = index_of(1 - row, 1 - col, core)
    p_x = index_of(row, 1 - col, 1 - core)
    p_y = index_of(1 - row, col, 1 - core)
    p_d = index_of(1 - row, 1 - col, 1 - core)
    r1, r2 = w1s.shape[1], w2s.shape[1]
    rows = h.shape[0]
    tiles = rows // tile

    greet((j_p, j_x, j_y))

    def part(which, slot, j):
        if which == 1:
            return w1.at[slot, pl.ds(pl.multiple_of(j * r1, r1), r1)]
        return w2.at[slot, pl.ds(pl.multiple_of(j * r2, r2), r2)]

    sends = (
        (1, me, j_y, j_y), (1, me, j_x, j_x), (1, me, j_p, j_p),
        (2, me, j_x, j_x), (2, me, j_y, j_y), (2, me, j_p, j_p),
        (1, j_y, j_x, j_d), (1, j_y, j_p, p_y), (2, j_x, j_y, j_d), (2, j_x, j_p, p_x),
        (1, j_x, j_p, p_x), (2, j_y, j_p, p_y),
        (1, j_d, j_p, p_d), (2, j_d, j_p, p_d),
    )

    def channel(layer, k, incoming=False):
        slot = layer % SLOTS
        which, out, to, inc = sends[k]
        ref = part(which, slot, inc if incoming else out)
        return pltpu.make_async_remote_copy(
            src_ref=ref, dst_ref=ref, send_sem=send_sem.at[slot, k], recv_sem=recv_sem.at[slot, k],
            device_id=(to,), device_id_type=MESH)

    def start(layer, ks):
        for k in ks:
            channel(layer, k).start()

    def arrive(layer, ks):
        for k in ks:
            channel(layer, k, True).wait_recv()

    def own(layer):
        st = layer % 2
        return (pltpu.make_async_copy(w1s.at[layer], s1_st.at[st], own_sem.at[st, 0]),
                pltpu.make_async_copy(w2s.at[layer], s2_st.at[st], own_sem.at[st, 1]))

    def place_own(layer):
        for copy in own(layer):
            copy.wait()
        part(1, layer % SLOTS, me)[...] = s1_st[layer % 2].astype(BF16)
        part(2, layer % SLOTS, me)[...] = s2_st[layer % 2].astype(BF16)

    def on(layer):
        return jnp.logical_and(layer >= 0, layer < layers)

    def gather(i):
        @pl.when(on(i + AHEAD_CORE))
        def _():
            arrive(i + AHEAD_CORE, (6, 8))
            start(i + AHEAD_CORE, (12, 13))

        @pl.when(on(i + AHEAD_RELAY))
        def _():
            arrive(i + AHEAD_RELAY, (0, 1, 3, 4))
            start(i + AHEAD_RELAY, (6, 8, 7, 9, 10, 11))

        @pl.when(on(i + AHEAD_OWN))
        def _():
            place_own(i + AHEAD_OWN)
            start(i + AHEAD_OWN, (0, 3, 1, 4, 2, 5))

        @pl.when(on(i + AHEAD_OWN + 2))
        def _():
            for copy in own(i + AHEAD_OWN + 2):
                copy.start()

    def saved(layer, t, st):
        cols = pl.ds(pl.multiple_of(t * tile, tile), tile)
        return (pltpu.make_async_copy(zt_st.at[st], zt_out.at[layer, :, cols], st_sem.at[st, 0]),
                pltpu.make_async_copy(at_st.at[st], at_out.at[layer, :, cols], st_sem.at[st, 1]),
                pltpu.make_async_copy(p_st.at[st], p_out.at[layer, cols], st_sem.at[st, 2]))

    def turned(layer):
        return (pltpu.make_async_copy(w1t_st, w1t_out.at[layer], wt_sem.at[0]),
                pltpu.make_async_copy(w2t_st, w2t_out.at[layer], wt_sem.at[1]))

    def compute(layer):
        slot = layer % SLOTS

        def one(t):
            where = pl.ds(t * tile, tile)
            h_val = h[where, :]
            a_val = h_val.astype(BF16)
            step = layer * tiles + t
            st = step % 2
            if train:
                @pl.when(step >= 2)
                def _():
                    for copy in saved((step - 2) // tiles, (step - 2) % tiles, st):
                        copy.wait()

                at_st[st] = a_val.T
            lows = []
            for c in range(0, w1.shape[2], CHUNK):
                cut = slice(c, c + CHUNK)
                u = jnp.dot(a_val, w1[slot, :, cut], preferred_element_type=F32)
                sq = u * u
                w = 0.5 * (1.0 + jnp.tanh(u * (GELU_C + (GELU_C * GELU_K) * sq)))
                z = u * w
                z_low = z.astype(BF16)
                lows.append(z_low)
                if train:
                    p_st[st, :, cut] = w + (z * (1.0 - w)) * (2.0 * GELU_C + (6.0 * GELU_C * GELU_K) * sq)
                    zt_st[st, cut, :] = z_low.T
            if train:
                for copy in saved(layer, t, st):
                    copy.start()
            z_low = jnp.concatenate(lows, axis=1)
            h[where, :] = h_val + jnp.dot(z_low, w2[slot], preferred_element_type=F32)

        one(0)
        gather(layer)
        for t in range(1, tiles):
            one(t)
        if train:
            @pl.when(layer >= 1)
            def _():
                for copy in turned(layer - 1):
                    copy.wait()

            w1t_st[...] = w1[slot].T
            w2t_st[...] = w2[slot].T
            for copy in turned(layer):
                copy.start()

    x_copy = pltpu.make_async_copy(x_in, xb, io_sem.at[0])
    x_copy.start()
    for layer in (0, 1):
        for copy in own(layer):
            copy.start()

    def widen(t, _):
        where = pl.ds(pl.multiple_of(t * 256, 256), 256)
        h[where, :] = xb[where, :].astype(F32)
        return 0

    def turn(n, _):
        i = n - AHEAD_OWN

        @pl.when(i < 0)
        def _():
            gather(i)

        @pl.when(i == -1)
        def _():
            x_copy.wait()
            lax.fori_loop(0, rows // 256, widen, 0)

        @pl.when(i >= 0)
        def _():
            arrive(i, (2, 5, 7, 9, 10, 11, 12, 13))
            compute(i)
            for k in range(len(sends)):
                channel(i, k).wait_send()

        return 0

    lax.fori_loop(0, layers + AHEAD_OWN, turn, 0)

    if train:
        last = layers * tiles
        for step in (last - 2, last - 1):
            for copy in saved(step // tiles, step % tiles, step % 2):
                copy.wait()
        for copy in turned(layers - 1):
            copy.wait()
        y_copy = pltpu.make_async_copy(y_in, xb, io_sem.at[0])
        y_copy.start()
        y_copy.wait()

        def close(t, _):
            where = pl.ds(pl.multiple_of(t * 256, 256), 256)
            h[where, :] = (h[where, :] - xb[where, :].astype(F32)) / scale
            return 0

        lax.fori_loop(0, rows // 256, close, 0)
    out_copy = pltpu.make_async_copy(h, d_out if train else h_out, io_sem.at[1])
    out_copy.start()
    out_copy.wait()


def forward(train, w1s, w2s, x, y=None, scale=None, tile=768, cid=0):
    layers, r1, d_ff = w1s.shape
    r2, d_model = w2s.shape[1:]
    rows = x.shape[0]
    sds = jax.ShapeDtypeStruct
    h_shape = sds((rows, d_model), F32)
    scratch = [
        pltpu.VMEM((SLOTS, d_model, d_ff), BF16), pltpu.VMEM((SLOTS, d_ff, d_model), BF16),
        pltpu.VMEM((rows, d_model), F32), pltpu.VMEM((rows, d_model), BF16),
        pltpu.VMEM((2, r1, d_ff), F32), pltpu.VMEM((2, r2, d_model), F32),
        pltpu.SemaphoreType.DMA((SLOTS, 14)), pltpu.SemaphoreType.DMA((SLOTS, 14)),
        pltpu.SemaphoreType.DMA((2, 2)), pltpu.SemaphoreType.DMA((2,)),
    ]
    out = h_shape
    args = (w1s, w2s, x)
    if train:
        out = (h_shape, sds((layers, d_ff, rows), BF16), sds((layers, d_model, rows), BF16),
               sds((layers, rows, d_ff), F32), sds((layers, d_ff, d_model), BF16), sds((layers, d_model, d_ff), BF16))
        args = (w1s, w2s, x, y)
        scratch += [
            pltpu.VMEM((2, d_ff, tile), BF16), pltpu.VMEM((2, d_model, tile), BF16), pltpu.VMEM((2, tile, d_ff), F32),
            pltpu.VMEM((d_ff, d_model), BF16), pltpu.VMEM((d_model, d_ff), BF16),
            pltpu.SemaphoreType.DMA((2, 3)), pltpu.SemaphoreType.DMA((2,)),
        ]
    return pl.pallas_call(
        functools.partial(forward_kernel, train, layers, tile, scale),
        out_shape=out,
        in_specs=[ANY] * len(args),
        out_specs=jax.tree.map(lambda _: ANY, out),
        scratch_shapes=scratch,
        compiler_params=pltpu.CompilerParams(collective_id=cid, has_side_effects=True, vmem_limit_bytes=60 * 2**20),
        name="fwd_train" if train else "fwd_eval",
    )(*args)


def backward_kernel(layers, *refs):
    (d_in, zt_in, at_in, p_in, w1t_in, w2t_in, g1_out, g2_out,
     d, db, r, zt, at, p, w1t, w2t, ga, gb, da, dbuf, sa, sb, ra, rb, ta, tb, fa, fb, oa, ob,
     in_sem, d_sem, xd_send, xd_recv, x1_send, x1_recv, x2_send, x2_recv, out_sem) = refs
    me, core, col, row = place()
    j_p = index_of(row, col, 1 - core)
    j_x = index_of(row, 1 - col, core)
    j_y = index_of(1 - row, col, core)
    n_d, n_r = da.shape[0], ra.shape[0]
    s1, s2 = ga.shape[4], gb.shape[4]

    greet((j_p, j_x, j_y))

    def loads(n):
        layer, s = layers - 1 - n, n % 2
        return tuple(
            pltpu.make_async_copy(src.at[layer], dst.at[s], in_sem.at[s, k])
            for k, (src, dst) in enumerate(((w2t_in, w2t), (p_in, p), (w1t_in, w1t), (zt_in, zt), (at_in, at))))

    def remote(src, dst, send, recv, to):
        return pltpu.make_async_remote_copy(
            src_ref=src, dst_ref=dst, send_sem=send, recv_sem=recv, device_id=(to,), device_id_type=MESH)

    def hop_d(n, k):
        g, s = n % 2, n % n_d
        src, dst = ((ga, da), (gb, dbuf))[k]
        return remote(src.at[g, 1 - core], dst.at[s], xd_send.at[s, k], xd_recv.at[s, k], j_p)

    def hop_1(n, k):
        g, s = n % 2, n % n_r
        src, dst, away, to = ((sa, ra, 1 - row, j_y), (sb, rb, 1 - col, j_x))[k]
        return remote(src.at[g, away], dst.at[s], x1_send.at[s, k], x1_recv.at[s, k], to)

    def hop_2(n, k):
        g, s = n % 2, n % n_r
        src, dst, away, to = ((ta, fa, 1 - col, j_x), (tb, fb, 1 - row, j_y))[k]
        return remote(src.at[g, away], dst.at[s], x2_send.at[s, k], x2_recv.at[s, k], to)

    def result(n, k):
        s = n % 2
        src, dst = ((oa, g1_out), (ob, g2_out))[k]
        return pltpu.make_async_copy(src.at[s], dst.at[layers - 1 - n], out_sem.at[s, k])

    def on(n):
        return jnp.logical_and(n >= 0, n < layers)

    def add(x, y):
        return (x.astype(F32) + y.astype(F32)).astype(BF16)

    def sum_core(m, k):
        @pl.when(on(m))
        def _():
            hop_d(m, k).wait()
            src, got, out = ((ga, da, sa), (gb, dbuf, sb))[k]
            out[m % 2] = add(src[m % 2, core], got[m % n_d])
            hop_1(m, k).start()

    def sum_first(m, k):
        @pl.when(on(m))
        def _():
            hop_1(m, k).wait()
            src, got, out, here = ((sa, ra, ta, row), (sb, rb, tb, col))[k]
            out[m % 2] = add(src[m % 2, here], got[m % n_r])
            hop_2(m, k).start()

    def sum_second(m, k):
        @pl.when(on(m))
        def _():
            @pl.when(m >= 2)
            def _():
                result(m - 2, k).wait()

            hop_2(m, k).wait()
            src, got, out, here = ((ta, fa, oa, col), (tb, fb, ob, row))[k]
            out[m % 2] = add(src[m % 2, here], got[m % n_r])
            result(m, k).start()

    def early(n):
        sum_second(n - 3, 1)
        sum_first(n - 2, 1)
        sum_core(n - 1, 0)

    def late(n):
        sum_second(n - 3, 0)
        sum_first(n - 2, 0)
        sum_core(n, 1)

    def out_grad(n):
        s, g = n % 2, n % 2
        db[...] = d[...].astype(BF16)
        val = jnp.dot(zt[s], db[...], preferred_element_type=F32).astype(BF16)
        for k in range(8):
            gb[g, k % 2, (k // 2) % 2, k // 4] = val[k * s2:(k + 1) * s2]

    def in_back(n):
        s = n % 2
        q = jnp.dot(db[...], w2t[s], preferred_element_type=F32)
        r[...] = (p[s] * q).astype(BF16)

        @pl.when(n < layers - 1)
        def _():
            d[...] = d[...] + jnp.dot(r[...], w1t[s], preferred_element_type=F32)

    def in_grad(n):
        s, g = n % 2, n % 2
        val = jnp.dot(at[s], r[...], preferred_element_type=F32).astype(BF16)
        for k in range(8):
            ga[g, k % 2, k // 4, (k // 2) % 2] = val[k * s1:(k + 1) * s1]

    d_copy = pltpu.make_async_copy(d_in, d, d_sem)
    d_copy.start()
    for copy in loads(0):
        copy.start()
    d_copy.wait()

    def turn(n, _):
        @pl.when(n < layers)
        def _():
            for copy in loads(n):
                copy.wait()

            @pl.when(n + 1 < layers)
            def _():
                for copy in loads(n + 1):
                    copy.start()

            out_grad(n)

        early(n)

        @pl.when(n < layers)
        def _():
            hop_d(n, 1).start()
            in_back(n)

        late(n)

        @pl.when(n < layers)
        def _():
            in_grad(n)
            hop_d(n, 0).start()

        return 0

    lax.fori_loop(0, layers + 3, turn, 0)
    for n in (layers - 2, layers - 1):
        for k in range(2):
            result(n, k).wait()


def backward(d0, zt, at, p, w1t, w2t, n_dev, cid=1):
    layers, d_ff, rows = zt.shape
    d_model = d0.shape[1]
    s1, s2 = d_model // n_dev, d_ff // n_dev
    sds = jax.ShapeDtypeStruct
    vm, sem = pltpu.VMEM, pltpu.SemaphoreType.DMA
    n_d, n_r = 2, 4
    scratch = [
        vm((rows, d_model), F32), vm((rows, d_model), BF16), vm((rows, d_ff), BF16),
        vm((2, d_ff, rows), BF16), vm((2, d_model, rows), BF16), vm((2, rows, d_ff), F32),
        vm((2, d_ff, d_model), BF16), vm((2, d_model, d_ff), BF16),
        vm((2, 2, 2, 2, s1, d_ff), BF16), vm((2, 2, 2, 2, s2, d_model), BF16),
        vm((n_d, 2, 2, s1, d_ff), BF16), vm((n_d, 2, 2, s2, d_model), BF16),
        vm((2, 2, 2, s1, d_ff), BF16), vm((2, 2, 2, s2, d_model), BF16),
        vm((n_r, 2, s1, d_ff), BF16), vm((n_r, 2, s2, d_model), BF16),
        vm((2, 2, s1, d_ff), BF16), vm((2, 2, s2, d_model), BF16),
        vm((n_r, s1, d_ff), BF16), vm((n_r, s2, d_model), BF16),
        vm((2, s1, d_ff), BF16), vm((2, s2, d_model), BF16),
        sem((2, 5)), sem(()), sem((n_d, 2)), sem((n_d, 2)), sem((n_r, 2)), sem((n_r, 2)),
        sem((n_r, 2)), sem((n_r, 2)), sem((2, 2)),
    ]
    return pl.pallas_call(
        functools.partial(backward_kernel, layers),
        out_shape=(sds((layers, s1, d_ff), BF16), sds((layers, s2, d_model), BF16)),
        in_specs=[ANY] * 6,
        out_specs=(ANY, ANY),
        scratch_shapes=scratch,
        compiler_params=pltpu.CompilerParams(collective_id=cid, has_side_effects=True, vmem_limit_bytes=63 * 2**20),
        name="bwd",
    )(d0, zt, at, p, w1t, w2t)


def solution(mesh):
    n_dev = mesh.shape["data"]
    w_spec = P(None, "data", None)
    row_spec = P("data", None)

    def device_step(w_one, w_two, mom_one, mom_two, x_zero, y_zero, x_one, y_one):
        tok_dev, d_model = x_zero.shape
        scale = float(n_dev * tok_dev * d_model)
        d0, zt, at, p, w1t, w2t = forward(True, w_one, w_two, x_zero, y_zero, scale, cid=0)
        g1, g2 = backward(d0, zt, at, p, w1t, w2t, n_dev, cid=1)
        new_mom_one = MOMENTUM * mom_one + g1.astype(F32)
        new_mom_two = MOMENTUM * mom_two + g2.astype(F32)
        new_w_one = w_one - LEARN_RATE * new_mom_one
        new_w_two = w_two - LEARN_RATE * new_mom_two
        h_last = forward(False, new_w_one, new_w_two, x_one, cid=2)
        loss_rows = jnp.sum(jnp.square(h_last - y_one.astype(F32)), axis=1) / (2 * d_model)
        return new_w_one, new_w_two, new_mom_one, new_mom_two, loss_rows, h_last

    return jax.shard_map(device_step, mesh=mesh, in_specs=(w_spec, w_spec, w_spec, w_spec, row_spec, row_spec, row_spec, row_spec), out_specs=(w_spec, w_spec, w_spec, w_spec, P("data"), row_spec), check_vma=False)
```

time: 982 us -> 907 us (0.924)
  Pallas kernels: 939 us -> 873 us
  other arithmetic: 38.1 us -> 26.2 us
    pallas_call x2, Pallas kernels: 630 us -> 581 us  [forward(): pl.pallas_call(functools.partial(forward_kernel, train, layers, tile, sca...]
    convert_element_type x4 -> x0, other arithmetic: 35.1 us -> none  [the longest x1 13.9 us: device_step(): new_w_one.astype(BF16)]
    sub x0 -> x2, other arithmetic: none -> 23.2 us  [the longest x1 14.5 us: device_step(): new_w_one = w_one - LEARN_RATE * new_mom_one]
    pallas_call x1, Pallas kernels: 309 us -> 292 us  [backward(): pl.pallas_call(functools.partial(backward_kernel, layers), out_shape=(sds...]
where the time goes in v2:
time: 907 us
  Pallas kernels  873 us (96%)
  other arithmetic  26.2 us (3%)
    pallas_call x2, Pallas kernels, forward(): pl.pallas_call(functools.partial(forward_kernel, train, layers, tile, sca...  581 us
    pallas_call x1, Pallas kernels, backward(): pl.pallas_call(functools.partial(backward_kernel, layers), out_shape=(sds...  292 us

profile of v2, /device:TPU:0, one launch (start us, length us, event | category | flops | bytes accessed | tf_op | source)
XLA Modules:
  0.0 907.0 jit_solution(397144558819307978)
XLA Ops:
  0.6 297.7 %fwd_train.1 = (f32[1536,512]{1,0:T(8,128)}, bf16[32,1024,1536]{2,1,0:T(8,128)(2,1)}, bf16[32,512,1536]{2,1,0:T(8,128)(2,1)}, f32[32,1536,1024]{2,1,0:T(8,128)},...) custom-call(f32[32,64,1024]{2,1,0:T(8,128)} %refs_0_.1, f32[32,128,512]{2,1,0:T(8,128)} %refs_1_.1, ...), custom_call_target="tpu_custom_call" | custom-call | tf_op jit(solution)/shard_map/fwd_train/pallas_call | solution.py:264
  298.4 292.3 %bwd.1 = (bf16[32,64,1024]{2,1,0:T(8,128)(2,1)}, bf16[32,128,512]{2,1,0:T(8,128)(2,1)}) custom-call(f32[1536,512]{1,0:T(8,128)} %get-tuple-element.14.refs_0_, bf16[32,1024,1536]{2,1,0:T(8,128)(2,1)} %get-tuple-element.15.refs_1_, bf16[32,512,1536]{2,1,0:T(8,128)(2,1)} %get-tuple-element.16.refs_2_, f32[32,1536,1024]{2,1,0:T(8,128)} %get-tuple-element.17.refs_3_, ...), custom_call_target="tpu_custom_call" | custom-call | tf_op jit(solution)/shard_map/bwd/pallas_call | solution.py:446
  590.7 0.0 copy-start
  590.7 0.0 copy-start.1
  590.7 14.5 %multiply_subtract_fusion.1 = (f32[32,64,1024]{2,1,0:T(8,128)}, f32[32,64,1024]{2,1,0:T(8,128)}) fusion(f32[32,64,1024]{2,1,0:T(8,128)} %refs_0_.1, bf16[32,64,1024]{2,1,0:T(8,128)(2,1)} %get-tuple-element.20, f32[32,64,1024]{2,1,0:T(8,128)} %param.10), kind=kLoop, calls=%fused_computation.2 | loop fusion | flops 10485760 | bytes 37748736 | tf_op jit(solution)/shard_map/sub | solution.py:469
  605.2 0.0 copy-done
  605.2 3.0 copy-done.1
  608.2 8.8 multiply_subtract_fusion
  617.0 0.0 copy-start.2
  617.0 283.2 %fwd_eval.1 = f32[1536,512]{1,0:T(8,128)} custom-call(f32[32,64,1024]{2,1,0:T(8,128)} %get-tuple-element.32.refs_0_, f32[32,128,512]{2,1,0:T(8,128)} %get-tuple-element.33.refs_1_, bf16[1536,512]{1,0:T(8,128)(2,1)} %refs_2_.3), custom_call_target="tpu_custom_call" | custom-call | tf_op jit(solution)/shard_map/fwd_eval/pallas_call | solution.py:264
  900.2 0.0 copy-done.2
  900.2 2.4 multiply_reduce_fusion
  902.6 0.6 broadcast_multiply_fusion
  903.2 3.9 copy.15
Async XLA Ops:
  590.7 14.5 %copy-start = (f32[32,128,512]{2,1,0:T(8,128)S(1)}, f32[32,128,512]{2,1,0:T(8,128)}, u32[]{:S(2)}) copy-start(f32[32,128,512]{2,1,0:T(8,128)} %refs_1_.1) | copy-start | bytes 25165828
  590.7 17.5 %copy-start.1 = (f32[32,128,512]{2,1,0:T(8,128)S(1)}, f32[32,128,512]{2,1,0:T(8,128)}, u32[]{:S(2)}) copy-start(f32[32,128,512]{2,1,0:T(8,128)} %param.11) | copy-start | bytes 25165828
  617.0 283.2 %copy-start.2 = (bf16[1536,512]{1,0:T(8,128)(2,1)S(1)}, bf16[1536,512]{1,0:T(8,128)(2,1)}, u32[]{:S(2)}) copy-start(bf16[1536,512]{1,0:T(8,128)(2,1)} %param.15) | copy-start | bytes 4718596
